TPU v7x, 32 devices: a whole 2x2x4 slice. The times are simulated.
32 devices in a mesh: kt: 8 (over z, y), tile: 4 (over x, core).
Axes of the slice: x: 2, y: 2, z: 4, core: 2. Of those that a mesh axis runs over, the one named last changes fastest.
Arguments:
- green_particle: bfloat16 [2, 64, 1024, 1024], P(None, 'kt', 'tile'), may hold values from -6 to 6
- green_hole: bfloat16 [2, 64, 1024, 1024], P(None, 'kt', 'tile'), may hold values from -6 to 6
- coulomb: bfloat16 [2, 64, 1024, 1024], P(None, 'kt'), may hold values from -3 to 3
Outputs:
- screened: float32 [2, 64, 1024, 1024], P(None, 'kt', 'tile')
All inputs are finite; a program needn't handle non-finite values.
Results may differ from a plain program's by a relative error of at most 0.0039.
Values may be sent and summed in bfloat16 or wider, within the bound.
No kernel may reach another device: no remote copies, remote signals or barrier semaphores. Data moves between devices by JAX's collectives and lax.ppermute only.
A program may use at most 192 MiB of HBM per device.

v0:
```python
import math
import jax
import jax.numpy as jnp
from jax import lax
from jax.sharding import PartitionSpec as P

KSIDE = 4
K = 64
HIGHEST = lax.Precision.HIGHEST


def phase_tables(points, side_count):
    point_index = jnp.arange(points, dtype=jnp.int32)
    digit_high = point_index // (side_count * side_count)
    digit_mid = point_index // side_count % side_count
    digit_low = point_index % side_count
    phase_turns = (
        digit_high[:, None] * digit_high[None, :]
        + digit_mid[:, None] * digit_mid[None, :]
        + digit_low[:, None] * digit_low[None, :]
    ) % side_count
    angles = phase_turns.astype(jnp.float32) * (2.0 * math.pi / side_count)
    return (jnp.cos(angles) / points, jnp.sin(angles) / points)


def to_cells(real_part, imag_part, cosine_table, sine_table):
    return (
        jnp.dot(cosine_table, real_part, precision=HIGHEST)
        - jnp.dot(sine_table, imag_part, precision=HIGHEST),
        jnp.dot(sine_table, real_part, precision=HIGHEST)
        + jnp.dot(cosine_table, imag_part, precision=HIGHEST),
    )


def to_momenta(real_part, imag_part, cosine_table, sine_table):
    return (
        jnp.dot(cosine_table, real_part, precision=HIGHEST)
        + jnp.dot(sine_table, imag_part, precision=HIGHEST),
        jnp.dot(cosine_table, imag_part, precision=HIGHEST)
        - jnp.dot(sine_table, real_part, precision=HIGHEST),
    )


def polarize(particle, hole_part):
    cosine_table, sine_table = phase_tables(K, KSIDE)
    part_real, part_imag = to_cells(
        particle[0].astype(jnp.float32), particle[1].astype(jnp.float32), cosine_table, sine_table
    )
    hole_real, hole_imag = to_cells(
        hole_part[0].astype(jnp.float32), hole_part[1].astype(jnp.float32), cosine_table, sine_table
    )
    cell_real = part_real * hole_real - part_imag * hole_imag
    cell_imag = part_real * hole_imag + part_imag * hole_real
    mom_real, mom_imag = to_momenta(cell_real, cell_imag, cosine_table, sine_table)
    return jnp.stack([mom_real, mom_imag]).astype(jnp.bfloat16)


def product_of(left_side, right_side):
    return jnp.einsum("kij,kjl->kil", left_side, right_side, preferred_element_type=jnp.float32)


def complex_batched(left_real, left_imag, right_real, right_imag):
    real_out = product_of(left_real, right_real) - product_of(left_imag, right_imag)
    imag_out = product_of(left_real, right_imag) + product_of(left_imag, right_real)
    return (real_out, imag_out)


def body(green_particle, green_hole, coulomb):
    tile_rows = green_particle.shape[2]
    moved_part, moved_hole = (
        lax.all_to_all(green_particle, "kt", split_axis=3, concat_axis=1, tiled=True),
        lax.all_to_all(green_hole, "kt", split_axis=3, concat_axis=1, tiled=True),
    )
    points = moved_part.shape[1]
    narrow = moved_part.shape[3]
    polar_q = polarize(
        moved_part.reshape(2, points, tile_rows * narrow),
        moved_hole.reshape(2, points, tile_rows * narrow),
    )
    polar_q = polar_q.reshape(2, points, tile_rows, narrow)
    polar_rows = lax.all_to_all(polar_q, "kt", split_axis=1, concat_axis=3, tiled=True)
    mid_real, mid_imag = complex_batched(polar_rows[0], polar_rows[1], coulomb[0], coulomb[1])
    mid_stack = jnp.stack([mid_real.astype(jnp.bfloat16), mid_imag.astype(jnp.bfloat16)])
    row_start = lax.axis_index("tile") * tile_rows
    coulomb_rows = lax.dynamic_slice_in_dim(coulomb, row_start, tile_rows, 2)
    segment = lax.all_gather(mid_stack, "tile", axis=2, tiled=True)
    left_real = coulomb_rows[0]
    left_imag = coulomb_rows[1]
    more_real, more_imag = complex_batched(left_real, left_imag, segment[0], segment[1])
    summed = jnp.stack([more_real, more_imag])
    return coulomb_rows.astype(jnp.float32) + summed


def solution(mesh):
    return jax.shard_map(
        body,
        mesh=mesh,
        in_specs=(
            P(None, "kt", "tile", None),
            P(None, "kt", "tile", None),
            P(None, "kt", None, None),
        ),
        out_specs=P(None, "kt", "tile", None),
        check_vma=False,
    )
```

profile of v0, /device:TPU:0, one launch (start us, length us, event | category | flops | bytes accessed | tf_op | source)
XLA Modules:
  0.0 1116.9 jit_solution(6014429570869471573)
XLA Ops:
  6.5 12.6 %copy.8 = bf16[2,8,256,1024]{2,1,0,3:T(8,128)(2,1)} copy(bf16[2,8,256,1024]{3,2,1,0:T(8,128)(2,1)} %param.3) | data formatting | bytes 16777216 | tf_op args[0]
  19.1 7.3 all-to-all-start
  26.4 12.5 %copy.10 = bf16[2,8,256,1024]{2,1,0,3:T(8,128)(2,1)} copy(bf16[2,8,256,1024]{3,2,1,0:T(8,128)(2,1)} %param.4) | data formatting | bytes 16777216 | tf_op args[1]
  38.9 170.7 %all-to-all-done = bf16[2,8,256,1024]{2,1,0,3:T(8,128)(2,1)} async-done(((bf16[2,8,256,1024]{2,1,0,3:T(8,128)(2,1)}), bf16[2,8,256,1024]{2,1,0,3:T(8,128)(2,1)}, u32[]{:S(2)}, u32[]{:S(2)}) %all-to-all-start) | async-done | bytes 8388640 | tf_op jit(solution)/shard_map/all_to_all | solution.py:71
  209.6 5.0 all-to-all-start.1
  214.6 0.0 all-gather.2.cloned.1.call-start
  214.7 12.5 %copy.9 = bf16[2,8,256,8,128]{4,2,1,3,0:T(8,128)(2,1)} copy(bf16[2,8,256,8,128]{2,1,0,4,3:T(8,128)(2,1)} %bitcast.1) | data formatting | bytes 16777216 | tf_op jit(solution)/shard_map/all_to_all | solution.py:71
  227.2 5.3 slice_bitcast_fusion.8
  232.5 14.0 %fusion.28 = f32[64,32768]{1,0:T(8,128)} fusion(bf16[8,8,256,128]{3,2,1,0:T(8,128)(2,1)S(1)} %get-tuple-element.12, s32[64]{0:T(128)S(1)} %get-tuple-element.13, s32[64]{0:T(128)S(1)} %get-tuple-element.14, s32[64]{0:T(128)S(1)} %and_select_fusion.3), kind=kOutput, calls=%fused_computation.48 | convolution fusion | flops 1610690560 | bytes 12583680 | tf_op jit(solution)/shard_map/dot_general | solution.py:30
  246.5 14.5 %fusion.30 = f32[64,32768]{1,0:T(8,128)} fusion(bf16[8,8,256,128]{3,2,1,0:T(8,128)(2,1)S(1)} %get-tuple-element.12, s32[64]{0:T(128)S(1)} %get-tuple-element.13, s32[64]{0:T(128)S(1)} %get-tuple-element.14, s32[64]{0:T(128)S(1)} %and_select_fusion.3), kind=kOutput, calls=%fused_computation.50 | convolution fusion | flops 1610690560 | bytes 12583680 | tf_op jit(solution)/shard_map/dot_general | solution.py:28
  261.0 135.8 %all-to-all-done.1 = bf16[2,8,256,1024]{2,1,0,3:T(8,128)(2,1)} async-done(((bf16[2,8,256,1024]{2,1,0,3:T(8,128)(2,1)}), bf16[2,8,256,1024]{2,1,0,3:T(8,128)(2,1)}, u32[]{:S(2)}, u32[]{:S(2)}) %all-to-all-start.1) | async-done | bytes 8388640 | tf_op jit(solution)/shard_map/all_to_all | solution.py:72
  396.9 12.2 %copy.11 = bf16[2,8,256,8,128]{4,2,1,3,0:T(8,128)(2,1)} copy(bf16[2,8,256,8,128]{2,1,0,4,3:T(8,128)(2,1)} %bitcast.3) | data formatting | bytes 16777216 | tf_op jit(solution)/shard_map/all_to_all | solution.py:72
  409.1 4.0 slice_bitcast_fusion.6
  413.1 5.4 fusion.22
  418.4 5.4 fusion.24
  423.9 0.0 slice-start.2
  423.9 14.6 %convolution_add_fusion = f32[64,32768]{1,0:T(8,128)} fusion(f32[64,32768]{1,0:T(8,128)S(1)} %fusion.22, bf16[8,8,256,128]{3,2,1,0:T(8,128)(2,1)S(1)} %get-tuple-element.9, s32[64]{0:T(128)S(1)} %get-tuple-element.13, s32[64]{0:T(128)S(1)} %get-tuple-element.14, s32[64]{0:T(128)S(1)} %and_select_fusion.3), kind=kOutput, calls=%fused_computation | convolution fusion | flops 1612787712 | bytes 20972288 | tf_op jit(solution)/shard_map/dot_general | solution.py:31
  438.5 14.7 %convolution_subtract_fusion = f32[64,32768]{1,0:T(8,128)} fusion(f32[64,32768]{1,0:T(8,128)S(1)} %fusion.24, bf16[8,8,256,128]{3,2,1,0:T(8,128)(2,1)S(1)} %get-tuple-element.9, s32[64]{0:T(128)S(1)} %get-tuple-element.13, s32[64]{0:T(128)S(1)} %get-tuple-element.14, s32[64]{0:T(128)S(1)} %and_select_fusion.3), kind=kOutput, calls=%fused_computation.2 | convolution fusion | flops 1612787712 | bytes 20972288 | tf_op jit(solution)/shard_map/dot_general | solution.py:29
  453.3 14.4 %convolution_subtract_fusion.1 = f32[64,32768]{1,0:T(8,128)} fusion(f32[64,32768]{1,0:T(8,128)S(1)} %bitcast.119, bf16[8,8,256,128]{3,2,1,0:T(8,128)(2,1)S(1)} %copy-done.1, s32[64]{0:T(128)S(1)} %get-tuple-element.13, s32[64]{0:T(128)S(1)} %get-tuple-element.14, s32[64]{0:T(128)S(1)} %and_select_fusion.3), kind=kOutput, calls=%fused_computation.3 | convolution fusion | flops 1612787712 | bytes 20972288 | tf_op jit(solution)/shard_map/dot_general | solution.py:29
  467.7 22.5 %multiply_subtract_fusion = (f32[64,32768]{1,0:T(8,128)}, f32[64,32768]{1,0:T(8,128)}) fusion(f32[64,32768]{1,0:T(8,128)} %convolution_add_fusion, f32[64,32768]{1,0:T(8,128)} %convolution_subtract_fusion.1, f32[64,32768]{1,0:T(8,128)} %convolution_subtract_fusion, f32[64,32768]{1,0:T(8,128)} %fusion.28, bf16[8,8,256,128]{3,2,1,0:T(8,128)(2,1)} %get-tuple-element.11, ...), kind=kOutput, calls=%fused_computation.35 | convolution fusion | flops 1625370624 | bytes 54526720 | tf_op jit(solution)/shard_map/dot_general | solution.py:31
  490.2 12.3 %fusion.50 = f32[64,32768]{1,0:T(8,128)} fusion(f32[64,32768]{1,0:T(8,128)} %get-tuple-element.5, s32[64]{0:T(128)S(1)} %get-tuple-element.13, s32[64]{0:T(128)S(1)} %get-tuple-element.14, s32[64]{0:T(128)S(1)} %and_select_fusion.3), kind=kOutput, calls=%fused_computation.77 | convolution fusion | flops 1610690560 | bytes 16777984 | tf_op jit(solution)/shard_map/dot_general | solution.py:37
  502.6 7.8 fusion.49
  510.3 0.0 slice-start.1
  510.3 12.9 %fusion.45 = bf16[8,8,256,128]{3,1,2,0:T(8,128)(2,1)} fusion(f32[64,32768]{1,0:T(8,128)} %fusion.50, f32[64,32768]{1,0:T(8,128)S(1)} %copy-done, s32[64]{0:T(128)S(1)} %get-tuple-element.13, s32[64]{0:T(128)S(1)} %get-tuple-element.14, s32[64]{0:T(128)S(1)} %and_select_fusion.3), kind=kOutput, calls=%fused_computation.67 | convolution fusion | flops 1614884864 | bytes 20972288 | tf_op jit(solution)/shard_map/dot_general | solution.py:38
  523.3 8.9 fusion.44
  532.2 1.2 copy.20
  533.3 0.5 bitcast_bitcast_fusion
  533.8 0.5 copy-done.2
  534.3 1.2 copy.19
  535.5 2.2 bitcast_bitcast_fusion.1
  537.7 6.4 pad_maximum_fusion
  544.1 187.9 %all_to_all.45 = bf16[2,64,256,128]{3,2,0,1:T(8,128)(2,1)} all-to-all(bf16[2,64,256,128]{3,2,0,1:T(8,128)(2,1)} %pad_maximum_fusion), channel_id=1, replica_groups=mesh['kt'=8,'tile'=4] {'kt'}, dimensions={1} | all-to-all | bytes 16777216 | tf_op jit(solution)/shard_map/all_to_all | solution.py:81
  732.0 13.9 %copy.56 = bf16[2,8,8,256,128]{4,1,3,2,0:T(8,128)(2,1)} copy(bf16[2,8,8,256,128]{4,3,0,2,1:T(8,128)(2,1)} %bitcast.123) | data formatting | bytes 16777216 | tf_op jit(solution)/shard_map/all_to_all | solution.py:81
  745.9 5.8 fusion.116
  751.6 7.3 squeeze.43
  759.0 7.4 squeeze.41
  766.4 15.1 %fusion.2 = f32[8,256,1024]{2,1,0:T(8,128)} fusion(bf16[8,256,1024]{2,1,0:T(8,128)(2,1)} %squeeze.41, bf16[2,8,1024,1024]{3,2,1,0:T(8,128)(2,1)} %param.5), kind=kOutput, calls=%fused_computation.11 | convolution fusion | flops 4294967296 | bytes 29360128 | tf_op jit(solution)/shard_map/kij,kjl->kil/dot_general | solution.py:59
  781.5 13.6 %fusion.4 = f32[8,256,1024]{2,1,0:T(8,128)} fusion(bf16[8,256,1024]{2,1,0:T(8,128)(2,1)S(1)} %copy-done.3, bf16[2,8,1024,1024]{3,2,1,0:T(8,128)(2,1)} %param.5), kind=kOutput, calls=%fused_computation.13 | convolution fusion | flops 4294967296 | bytes 29360128 | tf_op jit(solution)/shard_map/kij,kjl->kil/dot_general | solution.py:59
  795.1 14.8 %fusion.19 = bf16[1,8,256,1024]{3,2,1,0:T(8,128)(2,1)} fusion(f32[8,256,1024]{2,1,0:T(8,128)} %fusion.2, bf16[8,256,1024]{2,1,0:T(8,128)(2,1)S(1)} %copy-done.3, bf16[2,8,1024,1024]{3,2,1,0:T(8,128)(2,1)} %param.5), kind=kOutput, calls=%fused_computation.37 | convolution fusion | flops 4299161600 | bytes 33554432 | tf_op jit(solution)/shard_map/kij,kjl->kil/dot_general | solution.py:59
  809.9 13.7 %fusion.18 = bf16[1,8,256,1024]{3,2,1,0:T(8,128)(2,1)} fusion(f32[8,256,1024]{2,1,0:T(8,128)} %fusion.4, bf16[8,256,1024]{2,1,0:T(8,128)(2,1)} %squeeze.41, bf16[2,8,1024,1024]{3,2,1,0:T(8,128)(2,1)} %param.5), kind=kOutput, calls=%fused_computation.36 | convolution fusion | flops 4299161600 | bytes 33554432 | tf_op jit(solution)/shard_map/kij,kjl->kil/dot_general | solution.py:59
  823.6 6.4 pad_maximum_fusion.1
  830.0 0.0 all-gather.2.cloned.1.call-update
  830.0 200.5 %all-gather.2.cloned.1.call-done = bf16[2,8,1024,1024]{3,2,1,0:T(8,128)(2,1)} async-done(((bf16[2,8,256,1024]{3,2,1,0:T(8,128)(2,1)}), bf16[2,8,1024,1024]{3,2,1,0:T(8,128)(2,1)}) %all-gather.2.cloned.1.call-update) | async-done | bytes 33554448 | tf_op jit(solution)/shard_map/all_gather | solution.py:86
  1030.5 14.8 %fusion.11 = f32[8,256,1024]{2,1,0:T(8,128)} fusion(bf16[2,8,1024,1024]{3,2,1,0:T(8,128)(2,1)} %all-gather.2.cloned.1.call-done, bf16[2,8,1024,1024]{3,2,1,0:T(8,128)(2,1)} %param.5, s32[]{:T(128)S(6)} %select_n.170), kind=kOutput, calls=%fused_computation.20 | convolution fusion | flops 4294967296 | bytes 29360132 | tf_op jit(solution)/shard_map/kij,kjl->kil/dot_general | solution.py:59
  1045.3 15.0 %fusion.10 = f32[8,256,1024]{2,1,0:T(8,128)} fusion(bf16[2,8,1024,1024]{3,2,1,0:T(8,128)(2,1)} %all-gather.2.cloned.1.call-done, bf16[2,8,1024,1024]{3,2,1,0:T(8,128)(2,1)} %param.5, s32[]{:T(128)S(6)} %add.203, s32[]{:T(128)S(6)} %select_n.170), kind=kOutput, calls=%fused_computation.19 | convolution fusion | flops 4294967296 | bytes 29360136 | tf_op jit(solution)/shard_map/kij,kjl->kil/dot_general | solution.py:59
  1060.3 17.2 %add_bitcast_fusion = f32[1,8,256,1024]{3,2,1,0:T(8,128)} fusion(f32[8,256,1024]{2,1,0:T(8,128)} %fusion.10, bf16[2,8,1024,1024]{3,2,1,0:T(8,128)(2,1)} %all-gather.2.cloned.1.call-done, bf16[2,8,1024,1024]{3,2,1,0:T(8,128)(2,1)} %param.5, s32[]{:T(128)S(6)} %select_n.170), kind=kOutput, calls=%fused_computation.30 | convolution fusion | flops 4297064448 | bytes 37748740 | tf_op jit(solution)/shard_map/kij,kjl->kil/dot_general | solution.py:59
  1077.5 17.5 %subtract_bitcast_fusion = f32[1,8,256,1024]{3,2,1,0:T(8,128)} fusion(f32[8,256,1024]{2,1,0:T(8,128)} %fusion.11, bf16[2,8,1024,1024]{3,2,1,0:T(8,128)(2,1)} %all-gather.2.cloned.1.call-done, bf16[2,8,1024,1024]{3,2,1,0:T(8,128)(2,1)} %param.5, s32[]{:T(128)S(6)} %add.203, s32[]{:T(128)S(6)} %select_n.170), kind=kOutput, calls=%fused_computation.31 | convolution fusion | flops 4297064448 | bytes 37748744 | tf_op jit(solution)/shard_map/kij,kjl->kil/dot_general | solution.py:59
  1095.0 14.7 %maximum_add_fusion = f32[2,8,256,1024]{3,2,1,0:T(8,128)} fusion(f32[1,8,256,1024]{3,2,1,0:T(8,128)} %add_bitcast_fusion, f32[1,8,256,1024]{3,2,1,0:T(8,128)} %subtract_bitcast_fusion, bf16[2,8,1024,1024]{3,2,1,0:T(8,128)(2,1)} %param.5, s32[]{:T(128)S(6)} %select_n.170), kind=kLoop, calls=%fused_computation.10 | loop fusion | flops 12582912 | bytes 41943044 | tf_op jit(solution)/shard_map/add | solution.py:91
  (19 shorter events, 0.0 us)
Async XLA Ops:
  19.1 190.5 %all-to-all-start = ((bf16[2,8,256,1024]{2,1,0,3:T(8,128)(2,1)}), bf16[2,8,256,1024]{2,1,0,3:T(8,128)(2,1)}, u32[]{:S(2)}, u32[]{:S(2)}) async-start(bf16[2,8,256,1024]{2,1,0,3:T(8,128)(2,1)} %copy.8), calls=%async_computation | async-start | bytes 16777216 | tf_op jit(solution)/shard_map/all_to_all | solution.py:71
  209.6 187.3 %all-to-all-start.1 = ((bf16[2,8,256,1024]{2,1,0,3:T(8,128)(2,1)}), bf16[2,8,256,1024]{2,1,0,3:T(8,128)(2,1)}, u32[]{:S(2)}, u32[]{:S(2)}) async-start(bf16[2,8,256,1024]{2,1,0,3:T(8,128)(2,1)} %copy.10), calls=%async_computation.1 | async-start | bytes 16777216 | tf_op jit(solution)/shard_map/all_to_all | solution.py:72
  214.6 815.9 %all-gather.2.cloned.1.call-start = ((), (), s32[]{:S(2)}) async-start(), calls=%async_computation.3 | async-start | bytes 41943040 | tf_op jit(solution)/shard_map/all_gather | solution.py:86
  423.9 29.4 %slice-start.2 = ((s8[8388608]{0:T(1024)(128)(4,1)}), s8[4194304]{0:T(1024)(128)(4,1)S(1)}, s32[]{:S(2)}) async-start(s8[8388608]{0:T(1024)(128)(4,1)} %bitcast.118), calls=%async_computation.6 | async-start | bytes 8388608
  438.5 14.8 %copy-start.1 = (bf16[8,8,256,128]{3,2,1,0:T(8,128)(2,1)S(1)}, bf16[8,8,256,128]{3,2,1,0:T(8,128)(2,1)}, u32[]{:S(2)}) copy-start(bf16[8,8,256,128]{3,2,1,0:T(8,128)(2,1)} %get-tuple-element.11) | copy-start | bytes 12582916
  438.5 14.8 %slice-start.3 = ((s8[8388608]{0:T(1024)(128)(4,1)}), s8[4194304]{0:T(1024)(128)(4,1)S(1)}, s32[]{:S(2)}) async-start(s8[8388608]{0:T(1024)(128)(4,1)} %bitcast.118), calls=%async_computation.7 | async-start | bytes 8388608
  490.2 12.3 %copy-start = (f32[64,32768]{1,0:T(8,128)S(1)}, f32[64,32768]{1,0:T(8,128)}, u32[]{:S(2)}) copy-start(f32[64,32768]{1,0:T(8,128)} %get-tuple-element.6) | copy-start | bytes 25165828
  502.5 20.7 %slice-start = ((s8[8388608]{0:T(1024)(128)(4,1)}), s8[4194304]{0:T(1024)(128)(4,1)S(1)}, s32[]{:S(2)}) async-start(s8[8388608]{0:T(1024)(128)(4,1)} %bitcast.116), calls=%async_computation.4 | async-start | bytes 8388608
  510.3 12.9 %slice-start.1 = ((s8[8388608]{0:T(1024)(128)(4,1)}), s8[4194304]{0:T(1024)(128)(4,1)S(1)}, s32[]{:S(2)}) async-start(s8[8388608]{0:T(1024)(128)(4,1)} %bitcast.116), calls=%async_computation.5 | async-start | bytes 8388608
  532.1 2.2 copy-start.2
  766.4 15.1 %copy-start.3 = (bf16[8,256,1024]{2,1,0:T(8,128)(2,1)S(1)}, bf16[8,256,1024]{2,1,0:T(8,128)(2,1)}, u32[]{:S(2)}) copy-start(bf16[8,256,1024]{2,1,0:T(8,128)(2,1)} %squeeze.43) | copy-start | bytes 12582916
  809.9 13.8 %copy-start.4 = (bf16[1,8,256,1024]{3,2,1,0:T(8,128)(2,1)S(1)}, bf16[1,8,256,1024]{3,2,1,0:T(8,128)(2,1)}, u32[]{:S(2)}) copy-start(bf16[1,8,256,1024]{3,2,1,0:T(8,128)(2,1)} %fusion.19) | copy-start | bytes 12582916
Sparse Core Ops, SparseCore 0:
  830.1 200.3 all-gather.1
where the time goes:
time: 1120 us
  waiting for transfers between devices  507 us (45%)
  matrix products  269 us (24%)
  blocking collectives  188 us (17%)
  local copies, waits for them, and re-layouts  99 us (9%)
  other arithmetic  27.4 us (2%)
  between operations  14 us (1%)
  starting transfers between devices  12.4 us (1%)
    all_gather x1, waiting for transfers between devices, body(): segment = lax.all_gather(mid_stack, 'tile', axis=2, tiled=True)  201 us
    all_to_all x1, blocking collectives, body(): lax.all_to_all(polar_q, 'kt', split_axis=1, concat_axis=3, tiled=True)  188 us
    all_to_all x1, waiting for transfers between devices, body(): lax.all_to_all(green_particle, 'kt', split_axis=3, concat_axis=1, tiled=T...  171 us
    all_to_all x1, waiting for transfers between devices, body(): lax.all_to_all(green_hole, 'kt', split_axis=3, concat_axis=1, tiled=True)  136 us
    dot_general x8, matrix products, product_of(): jnp.einsum('kij,kjl->kil', left_side, right_side, preferred_element_type=...  122 us
    unnamed x24, local copies, waits for them, and re-layouts  37.2 us
    dot_general x2, matrix products, to_cells(): jnp.dot(cosine_table, imag_part, precision=HIGHEST)  37.1 us
    dot_general x2, matrix products, to_cells(): jnp.dot(sine_table, imag_part, precision=HIGHEST)  29.1 us
  transfers between devices with their start and end apart: 3, of which 3 were waited for; matrix products, arithmetic and copies ran while one was open for 5% of the time, Pallas kernels for 0%

commit v1 on v0

--- a/solution.py
+++ b/solution.py
@@ -83,7 +83,7 @@
     mid_stack = jnp.stack([mid_real.astype(jnp.bfloat16), mid_imag.astype(jnp.bfloat16)])
     row_start = lax.axis_index("tile") * tile_rows
     coulomb_rows = lax.dynamic_slice_in_dim(coulomb, row_start, tile_rows, 2)
-    segment = lax.all_gather(mid_stack, "tile", axis=2, tiled=True)
+    segment = jnp.concatenate(lax.all_gather(mid_stack, "tile"), axis=2)
     left_real = coulomb_rows[0]
     left_imag = coulomb_rows[1]
     more_real, more_imag = complex_batched(left_real, left_imag, segment[0], segment[1])

time: 1120 us -> 1190 us (1.062)
  local copies, waits for them, and re-layouts: 99 us -> 151 us
  matrix products: 269 us -> 286 us
    all_to_all x1, waiting for transfers between devices: 136 us -> 171 us  [body(): lax.all_to_all(green_hole, 'kt', split_axis=3, concat_axis=1, tiled=True)]
    all_to_all x1, waiting for transfers between devices: 171 us -> 136 us  [body(): lax.all_to_all(green_particle, 'kt', split_axis=3, concat_axis=1, tiled=T...]
    slice x0 -> x1, local copies, waits for them, and re-layouts: none -> 23.3 us  [body(): segment[0]]
    all_gather x0 -> x1, local copies, waits for them, and re-layouts: none -> 23.2 us  [body(): segment = jnp.concatenate(lax.all_gather(mid_stack, 'tile'), axis=2)]
    unnamed x24 -> x28, local copies, waits for them, and re-layouts: 37.2 us -> 42.9 us
where the time goes in v1:
time: 1190 us
  waiting for transfers between devices  507 us (43%)
  matrix products  286 us (24%)
  blocking collectives  188 us (16%)
  local copies, waits for them, and re-layouts  151 us (13%)
  other arithmetic  28.7 us (2%)
  between operations  14 us (1%)
  starting transfers between devices  12.3 us (1%)
    all_gather x1, waiting for transfers between devices, body(): segment = jnp.concatenate(lax.all_gather(mid_stack, 'tile'), axis=2)  200 us
    all_to_all x1, blocking collectives, body(): lax.all_to_all(polar_q, 'kt', split_axis=1, concat_axis=3, tiled=True)  188 us
    all_to_all x1, waiting for transfers between devices, body(): lax.all_to_all(green_hole, 'kt', split_axis=3, concat_axis=1, tiled=True)  171 us
    all_to_all x1, waiting for transfers between devices, body(): lax.all_to_all(green_particle, 'kt', split_axis=3, concat_axis=1, tiled=T...  136 us
    dot_general x8, matrix products, product_of(): jnp.einsum('kij,kjl->kil', left_side, right_side, preferred_element_type=...  121 us
    unnamed x28, local copies, waits for them, and re-layouts  42.9 us
    dot_general x2, matrix products, to_cells(): jnp.dot(cosine_table, imag_part, precision=HIGHEST)  37 us
    dot_general x2, matrix products, to_cells(): jnp.dot(sine_table, imag_part, precision=HIGHEST)  31.4 us
  transfers between devices with their start and end apart: 3, of which 3 were waited for; matrix products, arithmetic and copies ran while one was open for 5% of the time, Pallas kernels for 0%

profile of v1, /device:TPU:0, one launch (start us, length us, event | category | flops | bytes accessed | tf_op | source)
XLA Modules:
  0.0 1187.0 jit_solution(14686254979678681340)
XLA Ops:
  6.5 12.5 %copy.14 = bf16[2,8,256,1024]{2,1,0,3:T(8,128)(2,1)} copy(bf16[2,8,256,1024]{3,2,1,0:T(8,128)(2,1)} %param.4) | data formatting | bytes 16777216 | tf_op args[1]
  19.0 7.3 all-to-all-start.1
  26.3 12.6 %copy.12 = bf16[2,8,256,1024]{2,1,0,3:T(8,128)(2,1)} copy(bf16[2,8,256,1024]{3,2,1,0:T(8,128)(2,1)} %param.3) | data formatting | bytes 16777216 | tf_op args[0]
  39.0 170.6 %all-to-all-done.1 = bf16[2,8,256,1024]{2,1,0,3:T(8,128)(2,1)} async-done(((bf16[2,8,256,1024]{2,1,0,3:T(8,128)(2,1)}), bf16[2,8,256,1024]{2,1,0,3:T(8,128)(2,1)}, u32[]{:S(2)}, u32[]{:S(2)}) %all-to-all-start.1) | async-done | bytes 8388640 | tf_op jit(solution)/shard_map/all_to_all | solution.py:72
  209.5 5.0 all-to-all-start
  214.5 0.0 all-gather.3.cloned.1.call-start
  214.5 12.3 %copy.15 = bf16[2,8,256,8,128]{4,2,1,3,0:T(8,128)(2,1)} copy(bf16[2,8,256,8,128]{2,1,0,4,3:T(8,128)(2,1)} %bitcast.3) | data formatting | bytes 16777216 | tf_op jit(solution)/shard_map/all_to_all | solution.py:72
  226.8 5.3 slice_bitcast_fusion
  232.1 14.0 %fusion.20 = f32[64,32768]{1,0:T(8,128)} fusion(bf16[8,8,256,128]{3,2,1,0:T(8,128)(2,1)S(1)} %get-tuple-element.12, s32[64]{0:T(128)S(1)} %get-tuple-element.15, s32[64]{0:T(128)S(1)} %get-tuple-element.16, s32[64]{0:T(128)S(1)} %and_select_fusion.3), kind=kOutput, calls=%fused_computation.39 | convolution fusion | flops 1610690560 | bytes 12583680 | tf_op jit(solution)/shard_map/dot_general | solution.py:28
  246.1 14.6 %fusion.18 = f32[64,32768]{1,0:T(8,128)} fusion(bf16[8,8,256,128]{3,2,1,0:T(8,128)(2,1)S(1)} %get-tuple-element.12, s32[64]{0:T(128)S(1)} %get-tuple-element.15, s32[64]{0:T(128)S(1)} %get-tuple-element.16, s32[64]{0:T(128)S(1)} %and_select_fusion.3), kind=kOutput, calls=%fused_computation.37 | convolution fusion | flops 1610690560 | bytes 12583680 | tf_op jit(solution)/shard_map/dot_general | solution.py:30
  260.7 136.0 %all-to-all-done = bf16[2,8,256,1024]{2,1,0,3:T(8,128)(2,1)} async-done(((bf16[2,8,256,1024]{2,1,0,3:T(8,128)(2,1)}), bf16[2,8,256,1024]{2,1,0,3:T(8,128)(2,1)}, u32[]{:S(2)}, u32[]{:S(2)}) %all-to-all-start) | async-done | bytes 8388640 | tf_op jit(solution)/shard_map/all_to_all | solution.py:71
  396.7 12.3 %copy.13 = bf16[2,8,256,8,128]{4,2,1,3,0:T(8,128)(2,1)} copy(bf16[2,8,256,8,128]{2,1,0,4,3:T(8,128)(2,1)} %bitcast.1) | data formatting | bytes 16777216 | tf_op jit(solution)/shard_map/all_to_all | solution.py:71
  409.1 3.9 slice_bitcast_fusion.2
  413.0 14.3 %fusion.26 = f32[64,32768]{1,0:T(8,128)} fusion(bf16[8,8,256,128]{3,2,1,0:T(8,128)(2,1)S(1)} %get-tuple-element.14, s32[64]{0:T(128)S(1)} %get-tuple-element.15, s32[64]{0:T(128)S(1)} %get-tuple-element.16, s32[64]{0:T(128)S(1)} %and_select_fusion.3), kind=kOutput, calls=%fused_computation.45 | convolution fusion | flops 1610690560 | bytes 12583680 | tf_op jit(solution)/shard_map/dot_general | solution.py:28
  427.3 14.1 %fusion.24 = f32[64,32768]{1,0:T(8,128)} fusion(bf16[8,8,256,128]{3,2,1,0:T(8,128)(2,1)S(1)} %get-tuple-element.14, s32[64]{0:T(128)S(1)} %get-tuple-element.15, s32[64]{0:T(128)S(1)} %get-tuple-element.16, s32[64]{0:T(128)S(1)} %and_select_fusion.3), kind=kOutput, calls=%fused_computation.43 | convolution fusion | flops 1610690560 | bytes 12583680 | tf_op jit(solution)/shard_map/dot_general | solution.py:30
  441.4 14.7 %convolution_subtract_fusion = f32[64,32768]{1,0:T(8,128)} fusion(f32[64,32768]{1,0:T(8,128)S(1)} %bitcast.125, bf16[8,8,256,128]{3,2,1,0:T(8,128)(2,1)S(1)} %copy-done.2, s32[64]{0:T(128)S(1)} %get-tuple-element.15, s32[64]{0:T(128)S(1)} %get-tuple-element.16, s32[64]{0:T(128)S(1)} %and_select_fusion.3), kind=kOutput, calls=%fused_computation.2 | convolution fusion | flops 1612787712 | bytes 20972288 | tf_op jit(solution)/shard_map/dot_general | solution.py:29
  456.1 14.4 %convolution_add_fusion = f32[64,32768]{1,0:T(8,128)} fusion(f32[64,32768]{1,0:T(8,128)S(1)} %bitcast.123, bf16[8,8,256,128]{3,2,1,0:T(8,128)(2,1)S(1)} %copy-done.2, s32[64]{0:T(128)S(1)} %get-tuple-element.15, s32[64]{0:T(128)S(1)} %get-tuple-element.16, s32[64]{0:T(128)S(1)} %and_select_fusion.3), kind=kOutput, calls=%fused_computation | convolution fusion | flops 1612787712 | bytes 20972288 | tf_op jit(solution)/shard_map/dot_general | solution.py:31
  470.5 16.7 %convolution_subtract_fusion.1 = f32[64,32768]{1,0:T(8,128)} fusion(f32[64,32768]{1,0:T(8,128)} %fusion.26, bf16[8,8,256,128]{3,2,1,0:T(8,128)(2,1)S(1)} %get-tuple-element.13, s32[64]{0:T(128)S(1)} %get-tuple-element.15, s32[64]{0:T(128)S(1)} %get-tuple-element.16, s32[64]{0:T(128)S(1)} %and_select_fusion.3), kind=kOutput, calls=%fused_computation.3 | convolution fusion | flops 1612787712 | bytes 20972288 | tf_op jit(solution)/shard_map/dot_general | solution.py:29
  487.3 22.6 %multiply_subtract_fusion = (f32[64,32768]{1,0:T(8,128)}, f32[64,32768]{1,0:T(8,128)}) fusion(f32[64,32768]{1,0:T(8,128)} %convolution_add_fusion, f32[64,32768]{1,0:T(8,128)} %convolution_subtract_fusion.1, f32[64,32768]{1,0:T(8,128)} %convolution_subtract_fusion, f32[64,32768]{1,0:T(8,128)} %fusion.24, bf16[8,8,256,128]{3,2,1,0:T(8,128)(2,1)} %copy-done.1, ...), kind=kOutput, calls=%fused_computation.30 | convolution fusion | flops 1625370624 | bytes 54526720 | tf_op jit(solution)/shard_map/dot_general | solution.py:31
  509.8 10.4 fusion.50
  520.2 7.8 fusion.49
  528.0 10.6 fusion.45
  538.6 3.5 copy.24
  542.1 0.5 bitcast_bitcast_fusion.1
  542.6 1.7 slice-done.1
  544.3 10.4 fusion.44
  554.7 3.3 copy.25
  558.0 2.2 bitcast_bitcast_fusion
  560.3 6.4 pad_maximum_fusion
  566.7 187.9 %all_to_all.45 = bf16[2,64,256,128]{3,2,0,1:T(8,128)(2,1)} all-to-all(bf16[2,64,256,128]{3,2,0,1:T(8,128)(2,1)} %pad_maximum_fusion), channel_id=1, replica_groups=mesh['kt'=8,'tile'=4] {'kt'}, dimensions={1} | all-to-all | bytes 16777216 | tf_op jit(solution)/shard_map/all_to_all | solution.py:81
  754.6 13.9 %copy.63 = bf16[2,8,8,256,128]{4,1,3,2,0:T(8,128)(2,1)} copy(bf16[2,8,8,256,128]{4,3,0,2,1:T(8,128)(2,1)} %bitcast.129) | data formatting | bytes 16777216 | tf_op jit(solution)/shard_map/all_to_all | solution.py:81
  768.5 5.9 fusion.117
  774.3 7.3 squeeze.43
  781.6 7.4 squeeze.41
  789.1 15.0 %fusion.4 = f32[8,256,1024]{2,1,0:T(8,128)} fusion(bf16[8,256,1024]{2,1,0:T(8,128)(2,1)} %squeeze.43, bf16[2,8,1024,1024]{3,2,1,0:T(8,128)(2,1)} %param.5), kind=kOutput, calls=%fused_computation.12 | convolution fusion | flops 4294967296 | bytes 29360128 | tf_op jit(solution)/shard_map/kij,kjl->kil/dot_general | solution.py:59
  804.1 13.7 %fusion.2 = f32[8,256,1024]{2,1,0:T(8,128)} fusion(bf16[8,256,1024]{2,1,0:T(8,128)(2,1)S(1)} %copy-done.4, bf16[2,8,1024,1024]{3,2,1,0:T(8,128)(2,1)} %param.5), kind=kOutput, calls=%fused_computation.10 | convolution fusion | flops 4294967296 | bytes 29360128 | tf_op jit(solution)/shard_map/kij,kjl->kil/dot_general | solution.py:59
  817.8 13.4 %fusion.14 = bf16[1,8,256,1024]{3,2,1,0:T(8,128)(2,1)} fusion(f32[8,256,1024]{2,1,0:T(8,128)} %fusion.4, bf16[8,256,1024]{2,1,0:T(8,128)(2,1)} %squeeze.41, bf16[2,8,1024,1024]{3,2,1,0:T(8,128)(2,1)} %param.5), kind=kOutput, calls=%fused_computation.31 | convolution fusion | flops 4299161600 | bytes 33554432 | tf_op jit(solution)/shard_map/kij,kjl->kil/dot_general | solution.py:59
  831.2 14.8 %fusion.15 = bf16[1,8,256,1024]{3,2,1,0:T(8,128)(2,1)} fusion(f32[8,256,1024]{2,1,0:T(8,128)} %fusion.2, bf16[8,256,1024]{2,1,0:T(8,128)(2,1)S(1)} %copy-done.3, bf16[2,8,1024,1024]{3,2,1,0:T(8,128)(2,1)} %param.5), kind=kOutput, calls=%fused_computation.32 | convolution fusion | flops 4299161600 | bytes 33554432 | tf_op jit(solution)/shard_map/kij,kjl->kil/dot_general | solution.py:59
  845.9 7.6 pad_maximum_fusion.1
  853.6 0.0 all-gather.3.cloned.1.call-update
  853.6 200.4 %all-gather.3.cloned.1.call-done = bf16[8,8,256,1024]{3,2,1,0:T(8,128)(2,1)} async-done(((bf16[2,8,256,1024]{3,2,1,0:T(8,128)(2,1)}), bf16[8,8,256,1024]{3,2,1,0:T(8,128)(2,1)}) %all-gather.3.cloned.1.call-update) | async-done | bytes 33554448 | tf_op jit(solution)/shard_map/all_gather | solution.py:86
  1054.0 23.2 %copy.62 = bf16[4,2,8,256,1024]{4,3,0,2,1:T(8,128)(2,1)} copy(bf16[4,2,8,256,1024]{4,3,2,1,0:T(8,128)(2,1)} %bitcast.121) | data formatting | bytes 67108864 | tf_op jit(solution)/shard_map/all_gather | solution.py:86
  1077.3 23.3 %fusion.116 = (bf16[1,8,4,256,1024]{4,3,2,1,0:T(8,128)(2,1)}, bf16[1,8,4,256,1024]{4,3,2,1,0:T(8,128)(2,1)}) fusion(bf16[2,8,4,256,1024]{4,3,2,1,0:T(8,128)(2,1)} %bitcast.118), kind=kLoop, calls=%fused_computation.153 | loop fusion | bytes 67108864 | tf_op jit(solution)/shard_map/slice | solution.py:89
  1100.6 14.8 %fusion.37 = f32[8,256,1024]{2,1,0:T(8,128)} fusion(bf16[8,1024,1024]{2,1,0:T(8,128)(2,1)} %bitcast.114, bf16[2,8,1024,1024]{3,2,1,0:T(8,128)(2,1)} %param.5, s32[]{:T(128)S(6)} %select_n.170), kind=kOutput, calls=%fused_computation.62 | convolution fusion | flops 4294967296 | bytes 29360132 | tf_op jit(solution)/shard_map/kij,kjl->kil/dot_general | solution.py:59
  1115.4 14.8 %fusion.36 = f32[8,256,1024]{2,1,0:T(8,128)} fusion(bf16[8,1024,1024]{2,1,0:T(8,128)(2,1)} %bitcast.116, bf16[2,8,1024,1024]{3,2,1,0:T(8,128)(2,1)} %param.5, s32[]{:T(128)S(6)} %select_n.170), kind=kOutput, calls=%fused_computation.61 | convolution fusion | flops 4294967296 | bytes 29360132 | tf_op jit(solution)/shard_map/kij,kjl->kil/dot_general | solution.py:59
  1130.3 17.2 %subtract_bitcast_fusion = f32[1,8,256,1024]{3,2,1,0:T(8,128)} fusion(f32[8,256,1024]{2,1,0:T(8,128)} %fusion.37, bf16[8,1024,1024]{2,1,0:T(8,128)(2,1)} %bitcast.117, bf16[2,8,1024,1024]{3,2,1,0:T(8,128)(2,1)} %param.5, s32[]{:T(128)S(6)} %add.203, s32[]{:T(128)S(6)} %select_n.170), kind=kOutput, calls=%fused_computation.26 | convolution fusion | flops 4297064448 | bytes 37748744 | tf_op jit(solution)/shard_map/kij,kjl->kil/dot_general | solution.py:59
  1147.5 17.6 %add_bitcast_fusion = f32[1,8,256,1024]{3,2,1,0:T(8,128)} fusion(f32[8,256,1024]{2,1,0:T(8,128)} %fusion.36, bf16[8,1024,1024]{2,1,0:T(8,128)(2,1)} %bitcast.115, bf16[2,8,1024,1024]{3,2,1,0:T(8,128)(2,1)} %param.5, s32[]{:T(128)S(6)} %add.203, s32[]{:T(128)S(6)} %select_n.170), kind=kOutput, calls=%fused_computation.25 | convolution fusion | flops 4297064448 | bytes 37748744 | tf_op jit(solution)/shard_map/kij,kjl->kil/dot_general | solution.py:59
  1165.0 14.7 %maximum_add_fusion = f32[2,8,256,1024]{3,2,1,0:T(8,128)} fusion(f32[1,8,256,1024]{3,2,1,0:T(8,128)} %add_bitcast_fusion, f32[1,8,256,1024]{3,2,1,0:T(8,128)} %subtract_bitcast_fusion, bf16[2,8,1024,1024]{3,2,1,0:T(8,128)(2,1)} %param.5, s32[]{:T(128)S(6)} %select_n.170), kind=kLoop, calls=%fused_computation.9 | loop fusion | flops 12582912 | bytes 41943044 | tf_op jit(solution)/shard_map/add | solution.py:91
  (26 shorter events, 0.1 us)
Async XLA Ops:
  19.0 190.5 %all-to-all-start.1 = ((bf16[2,8,256,1024]{2,1,0,3:T(8,128)(2,1)}), bf16[2,8,256,1024]{2,1,0,3:T(8,128)(2,1)}, u32[]{:S(2)}, u32[]{:S(2)}) async-start(bf16[2,8,256,1024]{2,1,0,3:T(8,128)(2,1)} %copy.14), calls=%async_computation.1 | async-start | bytes 16777216 | tf_op jit(solution)/shard_map/all_to_all | solution.py:72
  209.5 187.2 %all-to-all-start = ((bf16[2,8,256,1024]{2,1,0,3:T(8,128)(2,1)}), bf16[2,8,256,1024]{2,1,0,3:T(8,128)(2,1)}, u32[]{:S(2)}, u32[]{:S(2)}) async-start(bf16[2,8,256,1024]{2,1,0,3:T(8,128)(2,1)} %copy.12), calls=%async_computation | async-start | bytes 16777216 | tf_op jit(solution)/shard_map/all_to_all | solution.py:71
  214.5 839.6 %all-gather.3.cloned.1.call-start = ((), (), s32[]{:S(2)}) async-start(), calls=%async_computation.3 | async-start | bytes 41943040 | tf_op jit(solution)/shard_map/all_gather | solution.py:86
  409.0 32.4 %slice-start.4 = ((s8[8388608]{0:T(1024)(128)(4,1)}), s8[4194304]{0:T(1024)(128)(4,1)S(1)}, s32[]{:S(2)}) async-start(s8[8388608]{0:T(1024)(128)(4,1)} %bitcast.124), calls=%async_computation.8 | async-start | bytes 8388608
  413.0 57.5 %copy-start.1 = (bf16[8,8,256,128]{3,2,1,0:T(8,128)(2,1)}, bf16[8,8,256,128]{3,2,1,0:T(8,128)(2,1)S(1)}, u32[]{:S(2)}) copy-start(bf16[8,8,256,128]{3,2,1,0:T(8,128)(2,1)S(1)} %get-tuple-element.13) | copy-start | bytes 12582916
  413.0 28.4 %slice-start.5 = ((s8[8388608]{0:T(1024)(128)(4,1)}), s8[4194304]{0:T(1024)(128)(4,1)S(1)}, s32[]{:S(2)}) async-start(s8[8388608]{0:T(1024)(128)(4,1)} %bitcast.124), calls=%async_computation.9 | async-start | bytes 8388608
  427.3 14.1 %copy-start.2 = (bf16[8,8,256,128]{3,2,1,0:T(8,128)(2,1)S(1)}, bf16[8,8,256,128]{3,2,1,0:T(8,128)(2,1)}, u32[]{:S(2)}) copy-start(bf16[8,8,256,128]{3,2,1,0:T(8,128)(2,1)} %get-tuple-element.11) | copy-start | bytes 12582916
  427.3 28.8 %slice-start.2 = ((s8[8388608]{0:T(1024)(128)(4,1)}), s8[4194304]{0:T(1024)(128)(4,1)S(1)}, s32[]{:S(2)}) async-start(s8[8388608]{0:T(1024)(128)(4,1)} %bitcast.122), calls=%async_computation.6 | async-start | bytes 8388608
  441.4 14.7 %slice-start.3 = ((s8[8388608]{0:T(1024)(128)(4,1)}), s8[4194304]{0:T(1024)(128)(4,1)S(1)}, s32[]{:S(2)}) async-start(s8[8388608]{0:T(1024)(128)(4,1)} %bitcast.122), calls=%async_computation.7 | async-start | bytes 8388608
  509.8 10.4 copy-start
  538.6 4.0 slice-start
  542.1 2.2 slice-start.1
  789.1 15.0 %copy-start.4 = (bf16[8,256,1024]{2,1,0:T(8,128)(2,1)S(1)}, bf16[8,256,1024]{2,1,0:T(8,128)(2,1)}, u32[]{:S(2)}) copy-start(bf16[8,256,1024]{2,1,0:T(8,128)(2,1)} %squeeze.41) | copy-start | bytes 12582916
  817.8 13.4 %copy-start.3 = (bf16[8,256,1024]{2,1,0:T(8,128)(2,1)S(1)}, bf16[8,256,1024]{2,1,0:T(8,128)(2,1)}, u32[]{:S(2)}) copy-start(bf16[8,256,1024]{2,1,0:T(8,128)(2,1)} %squeeze.43) | copy-start | bytes 12582916
Sparse Core Ops, SparseCore 0:
  853.7 200.2 all-gather.2
